TPU v7x, 32 devices: a whole 2x2x4 slice. The times are simulated.
32 devices in a mesh: grp: 2 (over x), seq: 8 (over z, y), kv: 2 (over core).
Axes of the slice: x: 2, y: 2, z: 4, core: 2. Of those that a mesh axis runs over, the one named last changes fastest.
Arguments:
- queries: bfloat16 [4, 64, 128], P(('grp', 'kv'), 'seq'), parts along dimension 0, may hold values from -256 to 256
- keys: bfloat16 [4, 16384, 8, 128], P(('grp', 'kv'), 'seq'), parts along dimension 0, may hold values from -6 to 6
- values: bfloat16 [4, 16384, 8, 128], P(('grp', 'kv'), 'seq'), parts along dimension 0, may hold values from -6 to 6
- picks: int32 [4, 64, 3], P(('grp', 'kv'), 'seq'), parts along dimension 0, may hold values from 0 to 31, as said below
- lengths: int32 [4], P(('grp', 'kv')), parts along dimension 0, may hold values from 8194 to 16384, as said below
Outputs:
- attended: bfloat16 [4, 64, 128], P(('grp', 'kv'), 'seq'), parts along dimension 0
There are 2 independent parts, one for each index of `grp`. A program takes and returns all parts, laid end to end along the dimension named above; each array names one. Nothing has to cross between parts.
Inputs may be any that keep to these rules, and one draw needn't show every extreme that they name: `picks`: each row of 3 holds distinct block numbers in ascending order; the last is the block that holds position lengths[b] - 1, the others lie before it. Position lengths[b] - 1 is never the first position of its block.
All inputs are finite; a program needn't handle non-finite values.
Results may differ from a plain program's by a relative error of at most 0.0046.
Values may be sent and summed in bfloat16 or wider, within the bound.
A program may use at most 64 MiB of HBM per device.

v0:
```python
import math

import jax
import jax.numpy as jnp
from jax import lax
from jax.sharding import PartitionSpec as P

BLOCK = 512


NEGATIVE = -1e30


def shards(queries, keys, values, picks, lengths):
    rows = queries.shape[0]
    head_dim = queries.shape[2]
    local_len = keys.shape[1]
    kv_heads = keys.shape[2]
    blocks_here = local_len // BLOCK
    seq_index = lax.axis_index("seq")
    all_queries, all_picks = (
        lax.all_gather(queries, "seq", axis=1, tiled=True),
        lax.all_gather(picks, "seq", axis=1, tiled=True),
    )
    heads = all_queries.shape[1]
    group = heads // kv_heads
    grouped = all_queries.reshape(rows, kv_heads, group, head_dim)
    scores = jnp.einsum("bkgd,btkd->bkgt", grouped, keys, preferred_element_type=jnp.float32) * (
        1.0 / math.sqrt(head_dim)
    )
    scores = scores.reshape(rows, kv_heads, group, blocks_here, BLOCK)
    block_ids = seq_index * blocks_here + jnp.arange(blocks_here, dtype=jnp.int32)
    chosen = jnp.any(all_picks[:, :, :, None] == block_ids[None, None, None, :], axis=2)
    chosen = chosen.reshape(rows, kv_heads, group, blocks_here)
    positions = block_ids[:, None] * BLOCK + jnp.arange(BLOCK, dtype=jnp.int32)[None, :]
    inside = positions[None, :, :] < lengths[:, None, None]
    live = jnp.logical_and(chosen[..., None], inside[:, None, None, :, :])
    masked = jnp.where(live, scores, -jnp.inf)
    any_live = jnp.any(live, axis=-1)
    safe_max = jnp.where(any_live, jnp.max(masked, axis=-1), NEGATIVE)
    weight = jnp.exp(masked - safe_max[..., None])
    block_total = jnp.sum(weight, axis=-1)
    rounded = weight.astype(jnp.bfloat16)
    blocked_values = values.reshape(rows, blocks_here, BLOCK, kv_heads, head_dim)
    block_out = jnp.einsum(
        "bkgnt,bntkd->bkgnd", rounded, blocked_values, preferred_element_type=jnp.float32
    )
    device_max = jnp.max(safe_max, axis=-1)
    coef = jnp.exp(safe_max - device_max[..., None])
    partial_out = jnp.sum(block_out * coef[..., None], axis=3).reshape(rows, heads, head_dim)
    partial_total = jnp.sum(block_total * coef, axis=-1).reshape(rows, heads)
    partial_max = device_max.reshape(rows, heads)
    came_out, came_max, came_total = (
        lax.all_to_all(partial_out[None], "seq", split_axis=2, concat_axis=0, tiled=True),
        lax.all_to_all(partial_max[None], "seq", split_axis=2, concat_axis=0, tiled=True),
        lax.all_to_all(partial_total[None], "seq", split_axis=2, concat_axis=0, tiled=True),
    )
    top = jnp.max(came_max, axis=0)
    rescale = jnp.exp(came_max - top[None])
    mine_out = jnp.sum(came_out * rescale[..., None], axis=0)
    mine_total = jnp.sum(came_total * rescale, axis=0)
    return (mine_out / mine_total[..., None]).astype(jnp.bfloat16)


def solution(mesh):
    return jax.shard_map(
        shards,
        mesh=mesh,
        in_specs=(
            P(("grp", "kv"), "seq", None),
            P(("grp", "kv"), "seq", None, None),
            P(("grp", "kv"), "seq", None, None),
            P(("grp", "kv"), "seq", None),
            P(("grp", "kv")),
        ),
        out_specs=P(("grp", "kv"), "seq", None),
        check_vma=False,
    )
```

profile of v0, /device:TPU:0, one launch (start us, length us, event | category | flops | bytes accessed | tf_op | source)
XLA Modules:
  0.0 97.5 jit_solution(2691425866918644044)
XLA Ops:
  0.7 0.8 copy.28
  1.4 28.1 %all_gather.7 = bf16[1,64,128]{2,1,0:T(8,128)(2,1)S(1)} all-gather(bf16[1,8,128]{2,1,0:T(8,128)(2,1)} %param.5), channel_id=1, replica_groups=mesh['grp'=2,'seq'=8,'kv'=2] {'seq'}, dimensions={1}, use_global_device_ids=true | all-gather | bytes 18432 | tf_op jit(solution)/shard_map/all_gather | solution.py:22
  29.5 30.6 %all_gather.6 = s32[1,64,3]{2,0,1:T(1,128)S(1)} all-gather(s32[1,8,3]{2,0,1:T(1,128)S(1)} %copy.28), channel_id=1, replica_groups=mesh['grp'=2,'seq'=8,'kv'=2] {'seq'}, dimensions={1}, use_global_device_ids=true | all-gather | bytes 864 | tf_op jit(solution)/shard_map/all_gather | solution.py:23
  60.1 0.1 copy.29
  60.1 0.1 compare_reduce_fusion
  60.2 0.1 and.40
  60.3 0.1 add_compare_fusion
  60.4 0.7 and_reduce_fusion
  61.1 3.4 %fusion.4 = f32[8,8,2048]{2,1,0:T(8,128)S(1)} fusion(bf16[2048,8,128]{2,1,0:T(8,128)(2,1)} %bitcast.31, bf16[1,64,128]{2,1,0:T(8,128)(2,1)S(1)} %all_gather.7), kind=kOutput, calls=%fused_computation.4 | convolution fusion | flops 33685504 | bytes 4734976 | tf_op jit(solution)/shard_map/bkgd,btkd->bkgt/dot_general | solution.py:28
  64.5 0.2 fusion.16
  64.8 0.7 broadcast_in_dim_reshape.13
  65.5 3.9 %all-to-all-start.1 = ((f32[1,1,64]{1,0,2:T(1,128)}), f32[1,1,64]{1,0,2:T(1,128)S(1)}, u32[]{:S(2)}, u32[]{:S(2)}) async-start(f32[1,1,64]{1,0,2:T(1,128)} %broadcast_in_dim_reshape.13), calls=%async_computation.1 | async-start | bytes 65536 | tf_op jit(solution)/shard_map/all_to_all | solution.py:55
  69.4 0.3 exponential_reduce_fusion
  69.7 0.7 broadcast_in_dim_reshape.14
  70.4 5.6 %all-to-all-done.1 = f32[1,1,64]{1,0,2:T(1,128)S(1)} async-done(((f32[1,1,64]{1,0,2:T(1,128)}), f32[1,1,64]{1,0,2:T(1,128)S(1)}, u32[]{:S(2)}, u32[]{:S(2)}) %all-to-all-start.1) | async-done | bytes 288 | tf_op jit(solution)/shard_map/all_to_all | solution.py:55
  76.1 3.3 %all-to-all-start.2 = ((f32[1,1,64]{1,0,2:T(1,128)}), f32[1,1,64]{1,0,2:T(1,128)S(1)}, u32[]{:S(2)}, u32[]{:S(2)}) async-start(f32[1,1,64]{1,0,2:T(1,128)} %broadcast_in_dim_reshape.14), calls=%async_computation.2 | async-start | bytes 65536 | tf_op jit(solution)/shard_map/all_to_all | solution.py:56
  79.4 4.1 %fusion.13 = f32[8,8,128]{2,1,0:T(8,128)} fusion(bf16[4,512,8,128]{3,2,1,0:T(8,128)(2,1)} %bitcast.34, f32[8,8,4,512]{3,1,2,0:T(8,128)S(1)} %bitcast.30, f32[8,8,4]{1,2,0:T(4,128)S(1)} %get-tuple-element.8, pred[4,512]{1,0:T(4,128)(4,1)S(1)} %add_compare_fusion, pred[8,8,4]{1,2,0:T(4,128)(4,1)S(1)} %copy.30, f32[8,8,4]{1,2,0:T(4,128)S(1)} %get-tuple-element.6), kind=kOutput, calls=%fused_computation.7 | convolution fusion | flops 34136064 | bytes 4755712 | tf_op jit(solution)/shard_map/bkgnt,bntkd->bkgnd/dot_general | solution.py:45
  83.5 0.6 reduce.12
  84.0 0.1 all_to_all.32
  84.1 0.1 all_to_all.35
  84.2 1.9 %all-to-all-done.2 = f32[1,1,64]{1,0,2:T(1,128)S(1)} async-done(((f32[1,1,64]{1,0,2:T(1,128)}), f32[1,1,64]{1,0,2:T(1,128)S(1)}, u32[]{:S(2)}, u32[]{:S(2)}) %all-to-all-start.2) | async-done | bytes 288 | tf_op jit(solution)/shard_map/all_to_all | solution.py:56
  86.0 4.1 %all-to-all-start = ((f32[1,1,64,128]{3,1,0,2:T(1,128)}), f32[1,1,64,128]{3,1,0,2:T(1,128)S(1)}, u32[]{:S(2)}, u32[]{:S(2)}) async-start(f32[1,1,64,128]{3,1,0,2:T(1,128)} %bitcast.10), calls=%async_computation | async-start | bytes 65536 | tf_op jit(solution)/shard_map/all_to_all | solution.py:54
  90.1 0.6 reduce.13
  90.7 0.1 all_to_all.34
  90.8 6.0 %all-to-all-done = f32[1,1,64,128]{3,1,0,2:T(1,128)S(1)} async-done(((f32[1,1,64,128]{3,1,0,2:T(1,128)}), f32[1,1,64,128]{3,1,0,2:T(1,128)S(1)}, u32[]{:S(2)}, u32[]{:S(2)}) %all-to-all-start) | async-done | bytes 32800 | tf_op jit(solution)/shard_map/all_to_all | solution.py:54
  96.8 0.1 multiply_reduce_fusion
  96.9 0.7 fusion.22
  (8 shorter events, 0.1 us)
Async XLA Ops:
  65.5 10.5 %all-to-all-start.1 = ((f32[1,1,64]{1,0,2:T(1,128)}), f32[1,1,64]{1,0,2:T(1,128)S(1)}, u32[]{:S(2)}, u32[]{:S(2)}) async-start(f32[1,1,64]{1,0,2:T(1,128)} %broadcast_in_dim_reshape.13), calls=%async_computation.1 | async-start | bytes 65536 | tf_op jit(solution)/shard_map/all_to_all | solution.py:55
  76.1 10.0 %all-to-all-start.2 = ((f32[1,1,64]{1,0,2:T(1,128)}), f32[1,1,64]{1,0,2:T(1,128)S(1)}, u32[]{:S(2)}, u32[]{:S(2)}) async-start(f32[1,1,64]{1,0,2:T(1,128)} %broadcast_in_dim_reshape.14), calls=%async_computation.2 | async-start | bytes 65536 | tf_op jit(solution)/shard_map/all_to_all | solution.py:56
  86.0 10.8 %all-to-all-start = ((f32[1,1,64,128]{3,1,0,2:T(1,128)}), f32[1,1,64,128]{3,1,0,2:T(1,128)S(1)}, u32[]{:S(2)}, u32[]{:S(2)}) async-start(f32[1,1,64,128]{3,1,0,2:T(1,128)} %bitcast.10), calls=%async_computation | async-start | bytes 65536 | tf_op jit(solution)/shard_map/all_to_all | solution.py:54
where the time goes:
time: 98 us; the launch traced here: 97.5 us
  blocking collectives  58.7 us (60%)
  waiting for transfers between devices  13.5 us (14%)
  starting transfers between devices  11.3 us (12%)
  matrix products  7.44 us (8%)
  other arithmetic  3.38 us (3%)
  local copies, waits for them, and re-layouts  2.59 us (3%)
    all_gather x1, blocking collectives, shards(): lax.all_gather(picks, 'seq', axis=1, tiled=True)  30.6 us
    all_gather x1, blocking collectives, shards(): lax.all_gather(queries, 'seq', axis=1, tiled=True)  28.1 us
    all_to_all x1, waiting for transfers between devices, shards(): lax.all_to_all(partial_out[None], 'seq', split_axis=2, concat_axis=0, til...  5.99 us
    all_to_all x1, waiting for transfers between devices, shards(): lax.all_to_all(partial_max[None], 'seq', split_axis=2, concat_axis=0, til...  5.64 us
    all_to_all x1, starting transfers between devices, shards(): lax.all_to_all(partial_out[None], 'seq', split_axis=2, concat_axis=0, til...  4.09 us
    dot_general x1, matrix products, shards(): jnp.einsum('bkgnt,bntkd->bkgnd', rounded, blocked_values, preferred_eleme...  4.05 us
    all_to_all x1, starting transfers between devices, shards(): lax.all_to_all(partial_max[None], 'seq', split_axis=2, concat_axis=0, til...  3.86 us
    dot_general x1, matrix products, shards(): jnp.einsum('bkgd,btkd->bkgt', grouped, keys, preferred_element_type=jnp.f...  3.38 us
  transfers between devices with their start and end apart: 3, of which 3 were waited for; matrix products, arithmetic and copies ran while one was open for 6% of the time, Pallas kernels for 0%

commit v1 on v0

v1 whole, which is shorter than its diff:
```python
import functools
import math

import jax
import jax.numpy as jnp
from jax import lax
from jax.experimental import pallas as pl
from jax.experimental.pallas import tpu as pltpu
from jax.sharding import PartitionSpec as P

BLOCK = 512
CHUNK = 512
NEGATIVE = -1e30


def kernel(
    n,
    kv_heads,
    lengths_ref,
    q_ref,
    picks_ref,
    k_hbm,
    v_hbm,
    out_ref,
    kbuf,
    vbuf,
    qbuf,
    pbuf,
    qall,
    pall,
    bias,
    sbuf,
    msg,
    came,
    k_sem,
    v_sem,
    own_sem,
    q_send,
    q_recv,
    p_send,
    p_recv,
    m_send,
    m_recv,
):
    me = lax.axis_index("seq")
    hl, hd = q_ref.shape[1], q_ref.shape[2]
    heads = n * hl
    group = heads // kv_heads
    span = BLOCK * kv_heads
    blocks_here = k_hbm.shape[0] // span
    factor = math.log2(math.e) / math.sqrt(hd)

    barrier = pltpu.get_barrier_semaphore()
    for d in range(1, n):
        pl.semaphore_signal(
            barrier, inc=1, device_id={"seq": lax.rem(me + d, n)}, device_id_type=pl.DeviceIdType.MESH
        )
    k_copies, v_copies = [], []
    for b in range(blocks_here):
        rows = pl.ds(b * span, span)
        k_copies.append(pltpu.make_async_copy(k_hbm.at[rows], kbuf.at[rows], k_sem.at[b]))
        v_copies.append(pltpu.make_async_copy(v_hbm.at[rows], vbuf.at[rows], v_sem.at[b]))
    for c in k_copies:
        c.start()
    own_q = pltpu.make_async_copy(q_ref.at[0], qbuf.at[me], own_sem.at[0])
    own_p = pltpu.make_async_copy(picks_ref.at[0], pbuf.at[me], own_sem.at[1])
    own_q.start()
    own_p.start()
    for c in v_copies:
        c.start()
    pl.semaphore_wait(barrier, n - 1)

    sends = []
    for d in range(1, n):
        peer = {"seq": lax.rem(me + d, n)}
        for src, dst, s_sem, r_sem in (
            (q_ref.at[0], qbuf.at[me], q_send.at[d], q_recv.at[d]),
            (picks_ref.at[0], pbuf.at[me], p_send.at[d], p_recv.at[d]),
        ):
            c = pltpu.make_async_remote_copy(
                src_ref=src,
                dst_ref=dst,
                send_sem=s_sem,
                recv_sem=r_sem,
                device_id=peer,
                device_id_type=pl.DeviceIdType.MESH,
            )
            c.start()
            sends.append(c)
    own_q.wait()
    own_p.wait()
    for c in sends:
        c.wait_recv()

    for p in range(n):
        qall[p * hl : (p + 1) * hl, :] = qbuf[p].astype(jnp.float32)
        pall[p * hl : (p + 1) * hl, :] = pbuf[p]
    q = qall[...].astype(jnp.bfloat16)
    picks = pall[...]
    length = lengths_ref[0]

    lane = lax.broadcasted_iota(jnp.int32, (heads, 128), 1)
    row = lax.broadcasted_iota(jnp.int32, (heads, 128), 0)
    mine = (lane % kv_heads) == (row // group)
    for b in range(blocks_here):
        block_id = me * blocks_here + b
        chosen = jnp.max((picks == block_id).astype(jnp.int32), axis=1, keepdims=True)
        ok = jnp.logical_and(mine, jnp.broadcast_to(chosen, (heads, 128)) > 0)
        bias[b] = jnp.where(ok, 0.0, NEGATIVE)

    reps = CHUNK // 128
    col = lax.broadcasted_iota(jnp.int32, (1, CHUNK), 1) // kv_heads
    dims = (((1,), (1,)), ((), ()))
    top = jnp.full((heads, 128), 3 * NEGATIVE, jnp.float32)
    for b in range(blocks_here):
        k_copies[b].wait()
        start = (me * blocks_here + b) * BLOCK
        for j in range(span // CHUNK):
            lo = b * span + j * CHUNK
            s = lax.dot_general(q, kbuf[lo : lo + CHUNK, :], dims, preferred_element_type=jnp.float32)
            end = jnp.where(col + (start + j * (CHUNK // kv_heads)) < length, 0.0, NEGATIVE)
            for r in range(reps):
                part = s[:, r * 128 : (r + 1) * 128] + (bias[b] + end[:, r * 128 : (r + 1) * 128])
                top = jnp.maximum(top, part)
                sbuf[:, lo + r * 128 : lo + (r + 1) * 128] = part
    high = jnp.max(top, axis=1, keepdims=True)
    high_wide = jnp.broadcast_to(high, (heads, 128))

    total = jnp.zeros((heads, 128), jnp.float32)
    acc = jnp.zeros((heads, hd), jnp.float32)
    for b in range(blocks_here):
        v_copies[b].wait()
        for j in range(span // CHUNK):
            lo = b * span + j * CHUNK
            pieces = []
            for r in range(reps):
                w = jnp.exp2((sbuf[:, lo + r * 128 : lo + (r + 1) * 128] - high_wide) * factor)
                total = total + w
                pieces.append(w.astype(jnp.bfloat16))
            acc = acc + jnp.dot(
                jnp.concatenate(pieces, axis=1), vbuf[lo : lo + CHUNK, :], preferred_element_type=jnp.float32
            )
    total_wide = jnp.broadcast_to(jnp.sum(total, axis=1, keepdims=True), (heads, 128))
    half = lax.broadcasted_iota(jnp.int32, (heads, 128), 1) < 64
    stats = jnp.where(half, high_wide, total_wide)
    for p in range(n):
        msg[p, 0] = acc[p * hl : (p + 1) * hl, :]
        msg[p, 1] = stats[p * hl : (p + 1) * hl, :]
    backs = []
    for d in range(1, n):
        peer = lax.rem(me + d, n)
        c = pltpu.make_async_remote_copy(
            src_ref=msg.at[peer],
            dst_ref=came.at[me],
            send_sem=m_send.at[d],
            recv_sem=m_recv.at[d],
            device_id={"seq": peer},
            device_id_type=pl.DeviceIdType.MESH,
        )
        c.start()
        backs.append(c)
    came[me] = msg[me]
    for c in sends:
        c.wait_send()
    for c in backs:
        c.wait_recv()
    best = came[0, 1]
    for p in range(1, n):
        best = jnp.maximum(best, came[p, 1])
    best = jnp.broadcast_to(best[:, 0:1], (hl, 128))
    sum_out = jnp.zeros((hl, hd), jnp.float32)
    sum_total = jnp.zeros((hl, 128), jnp.float32)
    for p in range(n):
        st = came[p, 1]
        scale = jnp.exp2((jnp.broadcast_to(st[:, 0:1], (hl, 128)) - best) * factor)
        sum_out = sum_out + came[p, 0] * scale
        sum_total = sum_total + jnp.broadcast_to(st[:, 64:65], (hl, 128)) * scale
    out_ref[0] = (sum_out / sum_total).astype(out_ref.dtype)
    for c in backs:
        c.wait_send()


def shards(n, queries, keys, values, picks, lengths):
    _, hl, hd = queries.shape
    _, local_len, kv_heads, _ = keys.shape
    heads = n * hl
    cols = local_len * kv_heads
    blocks_here = local_len // BLOCK
    k2 = keys.reshape(cols, hd)
    v2 = values.reshape(cols, hd)
    any_space = pl.BlockSpec(memory_space=pl.ANY)
    sems = [pltpu.SemaphoreType.DMA((n,)) for _ in range(6)]
    return pl.pallas_call(
        functools.partial(kernel, n, kv_heads),
        out_shape=jax.ShapeDtypeStruct((1, hl, hd), jnp.bfloat16),
        in_specs=[pl.BlockSpec(memory_space=pltpu.SMEM)] + [any_space] * 4,
        out_specs=pl.BlockSpec(memory_space=pltpu.VMEM),
        scratch_shapes=[
            pltpu.VMEM((cols, hd), jnp.bfloat16),
            pltpu.VMEM((cols, hd), jnp.bfloat16),
            pltpu.VMEM((n, hl, hd), jnp.bfloat16),
            pltpu.VMEM((n, hl, picks.shape[2]), jnp.int32),
            pltpu.VMEM((heads, hd), jnp.float32),
            pltpu.VMEM((heads, picks.shape[2]), jnp.int32),
            pltpu.VMEM((blocks_here, heads, 128), jnp.float32),
            pltpu.VMEM((heads, cols), jnp.float32),
            pltpu.VMEM((n, 2, hl, 128), jnp.float32),
            pltpu.VMEM((n, 2, hl, 128), jnp.float32),
            pltpu.SemaphoreType.DMA((blocks_here,)),
            pltpu.SemaphoreType.DMA((blocks_here,)),
            pltpu.SemaphoreType.DMA((2,)),
        ]
        + sems,
        compiler_params=pltpu.CompilerParams(collective_id=0, has_side_effects=True),
        name="block_attention",
    )(lengths, queries, picks, k2, v2)


def solution(mesh):
    return jax.shard_map(
        functools.partial(shards, mesh.shape["seq"]),
        mesh=mesh,
        in_specs=(
            P(("grp", "kv"), "seq", None),
            P(("grp", "kv"), "seq", None, None),
            P(("grp", "kv"), "seq", None, None),
            P(("grp", "kv"), "seq", None),
            P(("grp", "kv")),
        ),
        out_specs=P(("grp", "kv"), "seq", None),
        check_vma=False,
    )
```

time: 98 us -> 22.7 us (0.23)
  blocking collectives: 58.7 us -> 0 us
  Pallas kernels: 0 us -> 19.3 us
  waiting for transfers between devices: 13.5 us -> 0 us
  starting transfers between devices: 11.3 us -> 0 us
  matrix products: 7.44 us -> 0 us
  other arithmetic: 3.38 us -> 0 us
    all_gather x2 -> x0, blocking collectives: 58.7 us -> none  [the longest x1 30.6 us: shards(): lax.all_gather(picks, 'seq', axis=1, tiled=True)]
    pallas_call x0 -> x1, Pallas kernels: none -> 19.3 us  [shards(): pl.pallas_call(functools.partial(kernel, n, kv_heads), out_shape=jax.Shap...]
    all_to_all x3 -> x0, waiting for transfers between devices: 13.5 us -> none  [the longest x1 5.99 us: shards(): lax.all_to_all(partial_out[None], 'seq', split_axis=2, concat_axis=0, til...]
    all_to_all x3 -> x0, starting transfers between devices: 11.3 us -> none  [the longest x1 4.09 us: shards(): lax.all_to_all(partial_out[None], 'seq', split_axis=2, concat_axis=0, til...]
    dot_general x2 -> x0, matrix products: 7.44 us -> none  [the longest x1 4.05 us: shards(): jnp.einsum('bkgnt,bntkd->bkgnd', rounded, blocked_values, preferred_eleme...]
    unnamed x1 -> x2, local copies, waits for them, and re-layouts: 0.76 us -> 2.6 us
    another operation x2 -> x0, local copies, waits for them, and re-layouts: 1.42 us -> none  [the longest x1 0.71 us: shards(): partial_max[None]]
    all_to_all x2 -> x0, other arithmetic: 1.11 us -> none  [the longest x1 0.56 us: shards(): lax.all_to_all(partial_max[None], 'seq', split_axis=2, concat_axis=0, til...]
  transfers between devices with their start and end apart: 3 -> 0, of which waited for: 3 -> 0; matrix products, arithmetic and copies ran while one was open for 6% -> 0% of each run, Pallas kernels for 0% -> 0%
where the time goes in v1:
time: 22.7 us; the launch traced here: 22.6 us
  Pallas kernels  19.3 us (85%)
  local copies, waits for them, and re-layouts  2.6 us (11%)
  between operations  0.66 us (3%)
    pallas_call x1, Pallas kernels, shards(): pl.pallas_call(functools.partial(kernel, n, kv_heads), out_shape=jax.Shap...  19.3 us
    unnamed x2, local copies, waits for them, and re-layouts  2.6 us

profile of v1, /device:TPU:0, one launch (start us, length us, event | category | flops | bytes accessed | tf_op | source)
XLA Modules:
  0.0 22.6 jit_solution(8946553460041695419)
XLA Ops:
  0.7 1.3 %copy.6.picks_ref = s32[1,8,3]{2,1,0:T(8,128)} copy(s32[1,8,3]{1,0,2:T(1,128)} %param.8) | data formatting | bytes 192 | tf_op args[3]
  2.0 19.3 %block_attention.1 = bf16[1,8,128]{2,1,0:T(8,128)(2,1)} custom-call(s32[1]{0:T(128)S(6)} %copy.8.lengths_ref, bf16[1,8,128]{2,1,0:T(8,128)(2,1)} %q_ref.1, s32[1,8,3]{2,1,0:T(8,128)} %copy.6.picks_ref, bf16[16384,128]{1,0:T(8,128)(2,1)} %bitcast.2, bf16[16384,128]{1,0:T(8,128)(2,1)} %bitcast.3), custom_call_target="tpu_custom_call" | custom-call | tf_op jit(solution)/shard_map/block_attention/pallas_call | solution.py:193
  21.3 1.2 %copy.9 = bf16[1,8,128]{2,1,0:T(8,128)(2,1)} copy(bf16[1,8,128]{2,1,0:T(8,128)(2,1)} %block_attention.1) | data formatting | bytes 4096

commit v2 on v1

--- a/solution.py
+++ b/solution.py
@@ -28,6 +28,7 @@
     pbuf,
     qall,
     pall,
+    lbuf,
     bias,
     sbuf,
     msg,
@@ -63,19 +64,25 @@
     for c in k_copies:
         c.start()
     own_q = pltpu.make_async_copy(q_ref.at[0], qbuf.at[me], own_sem.at[0])
-    own_p = pltpu.make_async_copy(picks_ref.at[0], pbuf.at[me], own_sem.at[1])
+    own_p = pltpu.make_async_copy(picks_ref, pbuf.at[me], own_sem.at[1])
+    own_l = pltpu.make_async_copy(lengths_ref, lbuf, own_sem.at[2])
     own_q.start()
     own_p.start()
+    own_l.start()
     for c in v_copies:
         c.start()
+    pall[...] = jnp.full(pall.shape, -1, jnp.int32)
+    own_q.wait()
+    own_p.wait()
+    own_l.wait()
     pl.semaphore_wait(barrier, n - 1)
 
     sends = []
     for d in range(1, n):
         peer = {"seq": lax.rem(me + d, n)}
         for src, dst, s_sem, r_sem in (
-            (q_ref.at[0], qbuf.at[me], q_send.at[d], q_recv.at[d]),
-            (picks_ref.at[0], pbuf.at[me], p_send.at[d], p_recv.at[d]),
+            (qbuf.at[me], qbuf.at[me], q_send.at[d], q_recv.at[d]),
+            (pbuf.at[me], pbuf.at[me], p_send.at[d], p_recv.at[d]),
         ):
             c = pltpu.make_async_remote_copy(
                 src_ref=src,
@@ -87,17 +94,15 @@
             )
             c.start()
             sends.append(c)
-    own_q.wait()
-    own_p.wait()
     for c in sends:
         c.wait_recv()
 
     for p in range(n):
         qall[p * hl : (p + 1) * hl, :] = qbuf[p].astype(jnp.float32)
-        pall[p * hl : (p + 1) * hl, :] = pbuf[p]
+        pall[0 : pbuf.shape[1], p * hl : (p + 1) * hl] = pbuf[p, :, 0, :]
     q = qall[...].astype(jnp.bfloat16)
-    picks = pall[...]
-    length = lengths_ref[0]
+    picks = jnp.transpose(pall[...])[0:heads, :]
+    length = lbuf[0]
 
     lane = lax.broadcasted_iota(jnp.int32, (heads, 128), 1)
     row = lax.broadcasted_iota(jnp.int32, (heads, 128), 0)
@@ -192,28 +197,29 @@
     sems = [pltpu.SemaphoreType.DMA((n,)) for _ in range(6)]
     return pl.pallas_call(
         functools.partial(kernel, n, kv_heads),
-        out_shape=jax.ShapeDtypeStruct((1, hl, hd), jnp.bfloat16),
-        in_specs=[pl.BlockSpec(memory_space=pltpu.SMEM)] + [any_space] * 4,
+        out_shape=pltpu.VMEM((1, hl, hd), jnp.bfloat16),
+        in_specs=[pl.BlockSpec(memory_space=pltpu.HBM)] + [any_space] * 4,
         out_specs=pl.BlockSpec(memory_space=pltpu.VMEM),
         scratch_shapes=[
             pltpu.VMEM((cols, hd), jnp.bfloat16),
             pltpu.VMEM((cols, hd), jnp.bfloat16),
             pltpu.VMEM((n, hl, hd), jnp.bfloat16),
-            pltpu.VMEM((n, hl, picks.shape[2]), jnp.int32),
+            pltpu.VMEM((n, picks.shape[2], 1, hl), jnp.int32),
             pltpu.VMEM((heads, hd), jnp.float32),
-            pltpu.VMEM((heads, picks.shape[2]), jnp.int32),
+            pltpu.VMEM((8, 128), jnp.int32),
+            pltpu.SMEM((1,), jnp.int32),
             pltpu.VMEM((blocks_here, heads, 128), jnp.float32),
             pltpu.VMEM((heads, cols), jnp.float32),
             pltpu.VMEM((n, 2, hl, 128), jnp.float32),
             pltpu.VMEM((n, 2, hl, 128), jnp.float32),
             pltpu.SemaphoreType.DMA((blocks_here,)),
             pltpu.SemaphoreType.DMA((blocks_here,)),
-            pltpu.SemaphoreType.DMA((2,)),
+            pltpu.SemaphoreType.DMA((3,)),
         ]
         + sems,
         compiler_params=pltpu.CompilerParams(collective_id=0, has_side_effects=True),
         name="block_attention",
-    )(lengths, queries, picks, k2, v2)
+    )(lengths, queries, jnp.transpose(picks, (2, 0, 1)), k2, v2)
 
 
 def solution(mesh):

time: 22.7 us -> 20 us (0.88)
  local copies, waits for them, and re-layouts: 2.6 us -> 0.58 us
  Pallas kernels: 19.3 us -> 18.6 us
    unnamed x2 -> x1, local copies, waits for them, and re-layouts: 2.6 us -> 0.58 us
    pallas_call x1, Pallas kernels: 19.3 us -> 18.6 us  [shards(): pl.pallas_call(functools.partial(kernel, n, kv_heads), out_shape=pltpu.VM...]
where the time goes in v2:
time: 20 us; the launch traced here: 19.8 us
  Pallas kernels  18.6 us (93%)
  between operations  0.66 us (3%)
  local copies, waits for them, and re-layouts  0.58 us (3%)
    pallas_call x1, Pallas kernels, shards(): pl.pallas_call(functools.partial(kernel, n, kv_heads), out_shape=pltpu.VM...  18.6 us
    unnamed x1, local copies, waits for them, and re-layouts  0.58 us

profile of v2, /device:TPU:0, one launch (start us, length us, event | category | flops | bytes accessed | tf_op | source)
XLA Modules:
  0.0 19.8 jit_solution(12102984953578600013)
XLA Ops:
  0.7 18.6 %block_attention.1 = bf16[1,8,128]{2,1,0:T(8,128)(2,1)S(1)} custom-call(s32[1]{0:T(128)S(6)} %copy.8.lengths_ref, bf16[1,8,128]{2,1,0:T(8,128)(2,1)} %q_ref.1, s32[3,1,8]{2,1,0:T(1,128)} %bitcast.5, bf16[16384,128]{1,0:T(8,128)(2,1)} %bitcast.3, bf16[16384,128]{1,0:T(8,128)(2,1)} %bitcast.4), custom_call_target="tpu_custom_call" | custom-call | tf_op jit(solution)/shard_map/block_attention/pallas_call | solution.py:198
  19.2 0.6 %copy.7 = bf16[1,8,128]{2,1,0:T(8,128)(2,1)} copy(bf16[1,8,128]{2,1,0:T(8,128)(2,1)S(1)} %block_attention.1) | data formatting | bytes 4096

commit v3 on v2

v3 whole, which is shorter than its diff:
```python
import functools
import math

import jax
import jax.numpy as jnp
from jax import lax
from jax.experimental import pallas as pl
from jax.experimental.pallas import tpu as pltpu
from jax.sharding import PartitionSpec as P

BLOCK = 512
MIX = 256
NEGATIVE = -1e30


def kernel(
    n,
    kv_heads,
    lengths_ref,
    q_ref,
    picks_ref,
    k_hbm,
    v_hbm,
    out_ref,
    kbuf,
    vbuf,
    qbuf,
    pbuf,
    qall,
    pall,
    lbuf,
    khead,
    vhead,
    msg,
    came,
    k_sem,
    v_sem,
    own_sem,
    q_send,
    q_recv,
    p_send,
    p_recv,
    m_send,
    m_recv,
):
    me = lax.axis_index("seq")
    hl, hd = q_ref.shape[1], q_ref.shape[2]
    heads = n * hl
    group = heads // kv_heads
    span = BLOCK * kv_heads
    blocks_here = k_hbm.shape[0] // span
    factor = math.log2(math.e) / math.sqrt(hd)

    barrier = pltpu.get_barrier_semaphore()
    for d in range(1, n):
        pl.semaphore_signal(
            barrier, inc=1, device_id={"seq": lax.rem(me + d, n)}, device_id_type=pl.DeviceIdType.MESH
        )
    k_copies, v_copies = [], []
    for b in range(blocks_here):
        rows = pl.ds(b * span, span)
        k_copies.append(pltpu.make_async_copy(k_hbm.at[rows], kbuf.at[rows], k_sem.at[b]))
        v_copies.append(pltpu.make_async_copy(v_hbm.at[rows], vbuf.at[rows], v_sem.at[b]))
    for c in k_copies:
        c.start()
    own_q = pltpu.make_async_copy(q_ref.at[0], qbuf.at[me], own_sem.at[0])
    own_p = pltpu.make_async_copy(picks_ref, pbuf.at[me], own_sem.at[1])
    own_l = pltpu.make_async_copy(lengths_ref, lbuf, own_sem.at[2])
    own_q.start()
    own_p.start()
    own_l.start()
    for c in v_copies:
        c.start()
    pall[...] = jnp.full(pall.shape, -1, jnp.int32)
    own_q.wait()
    own_p.wait()
    own_l.wait()
    pl.semaphore_wait(barrier, n - 1)

    sends = {}
    for d in reversed(range(1, n)):
        peer = {"seq": lax.rem(me + d, n)}
        for name, buf, s_sem, r_sem in (("q", qbuf, q_send, q_recv), ("p", pbuf, p_send, p_recv)):
            c = pltpu.make_async_remote_copy(
                src_ref=buf.at[me],
                dst_ref=buf.at[me],
                send_sem=s_sem.at[d],
                recv_sem=r_sem.at[me],
                device_id=peer,
                device_id_type=pl.DeviceIdType.MESH,
            )
            c.start()
            sends[name, d] = c

    row = lax.broadcasted_iota(jnp.int32, (MIX, MIX), 0)
    lane = lax.broadcasted_iota(jnp.int32, (MIX, MIX), 1)
    tall = MIX // kv_heads
    perm = jnp.where(lane == (row % tall) * kv_heads + row // tall, 1.0, 0.0).astype(jnp.bfloat16)

    def regroup(src, dst, b):
        def step(i, carry):
            lo = pl.multiple_of(b * span + i * 2 * MIX, 2 * MIX)
            t0 = pl.multiple_of(b * BLOCK + i * 2 * tall, 2 * tall)
            x = jnp.concatenate([src[pl.ds(lo, MIX), :], src[pl.ds(lo + MIX, MIX), :]], axis=1)
            y = jnp.dot(perm, x, preferred_element_type=jnp.float32).astype(jnp.bfloat16)
            hd = src.shape[1]
            for k in range(kv_heads):
                dst[k, pl.ds(t0, tall), :] = y[k * tall : (k + 1) * tall, :hd]
                dst[k, pl.ds(t0 + tall, tall), :] = y[k * tall : (k + 1) * tall, hd:]
            return carry

        lax.fori_loop(0, span // (2 * MIX), step, 0, unroll=8)

    for b in range(blocks_here):
        k_copies[b].wait()
        regroup(kbuf, khead, b)
    for b in range(blocks_here):
        v_copies[b].wait()
        regroup(vbuf, vhead, b)

    length = lbuf[0]
    owners = group // hl
    local_len = blocks_here * BLOCK
    dims = (((1,), (1,)), ((), ()))
    wide = lax.broadcasted_iota(jnp.int32, (group, BLOCK), 1)
    half = lax.broadcasted_iota(jnp.int32, (group, 128), 1) < 64
    for k in range(kv_heads):
        for i in range(owners):
            p = k * owners + i

            @pl.when(p != me)
            def _():
                for buf, s_sem, r_sem in ((qbuf, q_send, q_recv), (pbuf, p_send, p_recv)):
                    pltpu.make_async_remote_copy(
                        src_ref=buf.at[p],
                        dst_ref=buf.at[p],
                        send_sem=s_sem.at[0],
                        recv_sem=r_sem.at[p],
                        device_id={"seq": lax.rem(me + 1, n)},
                        device_id_type=pl.DeviceIdType.MESH,
                    ).wait_recv()

            qall[k, i * hl : (i + 1) * hl, :] = qbuf[p].astype(jnp.float32)
            pall[k, 0 : pbuf.shape[1], i * hl : (i + 1) * hl] = pbuf[p, :, 0, :]
        q = qall[k].astype(jnp.bfloat16)
        picks = jnp.transpose(pall[k])[0:group, :]
        s = lax.dot_general(q, khead[k], dims, preferred_element_type=jnp.float32)
        parts = []
        high = jnp.full((group, 1), NEGATIVE, jnp.float32)
        for b in range(blocks_here):
            block_id = me * blocks_here + b
            chosen = jnp.max((picks == block_id).astype(jnp.int32), axis=1, keepdims=True)
            limit = jnp.where(chosen > 0, length - block_id * BLOCK, 0)
            part = jnp.where(wide < limit, s[:, b * BLOCK : (b + 1) * BLOCK], NEGATIVE)
            high = jnp.maximum(high, jnp.max(part, axis=1, keepdims=True))
            parts.append(part)
        w = jnp.exp2((jnp.concatenate(parts, axis=1) - high) * factor)
        total = jnp.sum(w, axis=1, keepdims=True)
        acc = jnp.dot(w.astype(jnp.bfloat16), vhead[k], preferred_element_type=jnp.float32)
        stats = jnp.where(half, jnp.broadcast_to(high, (group, 128)), jnp.broadcast_to(total, (group, 128)))
        for i in range(owners):
            p = k * owners + i
            msg[p, 0] = acc[i * hl : (i + 1) * hl, :]
            msg[p, 1] = stats[i * hl : (i + 1) * hl, :]

            @pl.when(p != me)
            def _():
                pltpu.make_async_remote_copy(
                    src_ref=msg.at[p],
                    dst_ref=came.at[me],
                    send_sem=m_send.at[p],
                    recv_sem=m_recv.at[me],
                    device_id={"seq": p},
                    device_id_type=pl.DeviceIdType.MESH,
                ).start()

    def back(d):
        p = lax.rem(me + d, n)
        return pltpu.make_async_remote_copy(
            src_ref=msg.at[p],
            dst_ref=came.at[p],
            send_sem=m_send.at[p],
            recv_sem=m_recv.at[p],
            device_id={"seq": p},
            device_id_type=pl.DeviceIdType.MESH,
        )

    backs = [back(d) for d in range(1, n)]
    came[me] = msg[me]
    for c in sends.values():
        c.wait_send()
    for c in backs:
        c.wait_recv()
    best = came[0, 1]
    for p in range(1, n):
        best = jnp.maximum(best, came[p, 1])
    best = jnp.broadcast_to(best[:, 0:1], (hl, 128))
    sum_out = jnp.zeros((hl, hd), jnp.float32)
    sum_total = jnp.zeros((hl, 128), jnp.float32)
    for p in range(n):
        st = came[p, 1]
        scale = jnp.exp2((jnp.broadcast_to(st[:, 0:1], (hl, 128)) - best) * factor)
        sum_out = sum_out + came[p, 0] * scale
        sum_total = sum_total + jnp.broadcast_to(st[:, 64:65], (hl, 128)) * scale
    out_ref[0] = (sum_out / sum_total).astype(out_ref.dtype)
    for c in backs:
        c.wait_send()


def shards(n, queries, keys, values, picks, lengths):
    _, hl, hd = queries.shape
    _, local_len, kv_heads, _ = keys.shape
    heads = n * hl
    cols = local_len * kv_heads
    blocks_here = local_len // BLOCK
    k2 = keys.reshape(cols, hd)
    v2 = values.reshape(cols, hd)
    any_space = pl.BlockSpec(memory_space=pl.ANY)
    sems = [pltpu.SemaphoreType.DMA((n,)) for _ in range(6)]
    return pl.pallas_call(
        functools.partial(kernel, n, kv_heads),
        out_shape=pltpu.VMEM((1, hl, hd), jnp.bfloat16),
        in_specs=[pl.BlockSpec(memory_space=pltpu.HBM)] + [any_space] * 4,
        out_specs=pl.BlockSpec(memory_space=pltpu.VMEM),
        scratch_shapes=[
            pltpu.VMEM((cols, hd), jnp.bfloat16),
            pltpu.VMEM((cols, hd), jnp.bfloat16),
            pltpu.VMEM((n, hl, hd), jnp.bfloat16),
            pltpu.VMEM((n, picks.shape[2], 1, hl), jnp.int32),
            pltpu.VMEM((kv_heads, heads // kv_heads, hd), jnp.float32),
            pltpu.VMEM((kv_heads, 8, 128), jnp.int32),
            pltpu.SMEM((1,), jnp.int32),
            pltpu.VMEM((kv_heads, local_len, hd), jnp.bfloat16),
            pltpu.VMEM((kv_heads, local_len, hd), jnp.bfloat16),
            pltpu.VMEM((n, 2, hl, 128), jnp.float32),
            pltpu.VMEM((n, 2, hl, 128), jnp.float32),
            pltpu.SemaphoreType.DMA((blocks_here,)),
            pltpu.SemaphoreType.DMA((blocks_here,)),
            pltpu.SemaphoreType.DMA((3,)),
        ]
        + sems,
        compiler_params=pltpu.CompilerParams(collective_id=0, has_side_effects=True),
        name="block_attention",
    )(lengths, queries, jnp.transpose(picks, (2, 0, 1)), k2, v2)


def solution(mesh):
    return jax.shard_map(
        functools.partial(shards, mesh.shape["seq"]),
        mesh=mesh,
        in_specs=(
            P(("grp", "kv"), "seq", None),
            P(("grp", "kv"), "seq", None, None),
            P(("grp", "kv"), "seq", None, None),
            P(("grp", "kv"), "seq", None),
            P(("grp", "kv")),
        ),
        out_specs=P(("grp", "kv"), "seq", None),
        check_vma=False,
    )
```

time: 20 us -> 17.1 us (0.86)
  Pallas kernels: 18.6 us -> 15.7 us
    pallas_call x1, Pallas kernels: 18.6 us -> 15.7 us  [shards(): pl.pallas_call(functools.partial(kernel, n, kv_heads), out_shape=pltpu.VM...]
where the time goes in v3:
time: 17.1 us; the launch traced here: 16.9 us
  Pallas kernels  15.7 us (92%)
  between operations  0.66 us (4%)
  local copies, waits for them, and re-layouts  0.58 us (3%)
    pallas_call x1, Pallas kernels, shards(): pl.pallas_call(functools.partial(kernel, n, kv_heads), out_shape=pltpu.VM...  15.7 us
    unnamed x1, local copies, waits for them, and re-layouts  0.58 us

profile of v3, /device:TPU:0, one launch (start us, length us, event | category | flops | bytes accessed | tf_op | source)
XLA Modules:
  0.0 16.9 jit_solution(5795192592833710319)
XLA Ops:
  0.7 15.7 %block_attention.1 = bf16[1,8,128]{2,1,0:T(8,128)(2,1)S(1)} custom-call(s32[1]{0:T(128)S(6)} %copy.8.lengths_ref, bf16[1,8,128]{2,1,0:T(8,128)(2,1)} %q_ref.1, s32[3,1,8]{2,1,0:T(1,128)} %bitcast.5, bf16[16384,128]{1,0:T(8,128)(2,1)} %bitcast.3, bf16[16384,128]{1,0:T(8,128)(2,1)} %bitcast.4), custom_call_target="tpu_custom_call" | custom-call | tf_op jit(solution)/shard_map/block_attention/pallas_call | solution.py:220
  16.3 0.6 %copy.7 = bf16[1,8,128]{2,1,0:T(8,128)(2,1)} copy(bf16[1,8,128]{2,1,0:T(8,128)(2,1)S(1)} %block_attention.1) | data formatting | bytes 4096
